TPU v7x, 256 devices: a whole 4x4x8 slice. The times are simulated.
256 devices in a mesh: band: 64 (over z, y_hi, x), ga: 4 (over y_lo, core).
Axes of the slice: x: 4, y: 4 (y_hi: 2, y_lo: 2; y = y_hi * 2 + y_lo), z: 8, core: 2. Of those that a mesh axis runs over, the one named last changes fastest.
Arguments:
- elements: bfloat16 [2, 6144, 2048], P(None, 'band', 'ga'), may hold values from -0.75 to 0.75
- screened: bfloat16 [2, 2, 2048, 2048], P(None, None, 'ga'), may hold values from -0.09375 to 0.09375
- energies: float32 [6144], replicated, may hold values from -3 to 3
- freq_points: float32 [2], replicated, may hold values from -3 to 3
- freq_weights: float32 [2], replicated, may hold values from 0.5 to 2
- band_of_slot: int32 [6144], replicated, may hold values from 0 to 6143, each once
Outputs:
- sigma: float32 [2, 6144, 6144], P(None, 'band', 'ga')
Inputs may be any that keep to these rules, and one draw needn't show every extreme that they name: `band_of_slot`: each of 0 to 6143 stands once.
All inputs are finite; a program needn't handle non-finite values.
Results may differ from a plain program's by a relative error of at most 0.0042.
Values may be sent and summed in bfloat16 or wider, within the bound.
A program may use at most 128 MiB of HBM per device.

v0:
```python
import jax
import jax.numpy as jnp
from jax import lax
from jax.sharding import Mesh
from jax.sharding import PartitionSpec as P

GA = ("ga_0", "ga_1")


def in_order(blocks, dim):
    shape = list(blocks.shape[1:])
    shape[dim] *= blocks.shape[0]
    return jnp.moveaxis(blocks, 0, dim).reshape(shape)


def all_blocks(shard, axes, order):
    blocks = shard
    for k in order:
        blocks = lax.all_gather(blocks, axes[k])
    done = order[::-1]
    back = [done.index(k) for k in range(len(axes))]
    blocks = blocks.transpose(*back, *range(len(axes), blocks.ndim))
    return blocks.reshape(-1, *shard.shape)


def gathered_by_axis(shard, axes, order, dim):
    return in_order(all_blocks(shard, axes, order), dim)


def split_up(shard, dim, peers):
    shape = shard.shape
    blocks = shard.reshape(*shape[:dim], peers, shape[dim] // peers, *shape[dim + 1 :])
    return jnp.moveaxis(blocks, dim, 0)


def summed_on_arrival(shard, axis, dim):
    blocks = split_up(shard, dim, lax.axis_size(axis))
    arrived = lax.all_to_all(blocks, axis, split_axis=0, concat_axis=0, tiled=True)
    return arrived.astype(jnp.float32).sum(axis=0)


def make_left(block):
    flipped = jnp.stack([-block[1], block[0]])
    return jnp.stack([block, flipped])


def on_device(elements, screened, energies, freq_points, freq_weights, band_of_slot):
    bands = elements.shape[1]
    slot_energy = jnp.take(energies, band_of_slot)
    offset = slot_energy[None, :] - freq_points[:, None]
    screen = freq_weights[:, None] / (1.0 + 4.0 * offset * offset)
    own_start = lax.axis_index("band") * bands
    screen_own = lax.dynamic_slice_in_dim(screen, own_start, bands, 1)
    piece = gathered_by_axis(elements, GA, (0, 1), 2)
    real_side = jnp.stack([piece[0], -piece[1]])
    imag_side = jnp.stack([piece[1], piece[0]])
    sides = jnp.stack([real_side, imag_side])
    applied = jnp.einsum(
        "dcmk,wcgk->wdmg", sides, screened, preferred_element_type=jnp.float32
    ).astype(jnp.bfloat16)
    left_own = make_left(elements)
    pairs = jnp.einsum(
        "dcnk,wcmk->wdnm",
        left_own,
        lax.all_gather(applied, "band", axis=2, tiled=True),
        preferred_element_type=jnp.float32,
    )
    factor = 0.5 * (screen_own[:, :, None] + screen[:, None, :])
    partial_rows = jnp.sum(pairs * factor[:, None], axis=0)
    return summed_on_arrival(partial_rows.astype(jnp.bfloat16), GA, 2)


def solution(mesh):
    torus = Mesh(mesh.devices.reshape(mesh.shape["band"], 2, 2), ("band", "ga_0", "ga_1"))
    return jax.shard_map(
        on_device,
        mesh=torus,
        in_specs=(P(None, "band", GA), P(None, None, GA, None), P(), P(), P(), P()),
        out_specs=P(None, "band", GA),
        check_vma=False,
    )
```

profile of v0, /device:TPU:1, one launch (start us, length us, event | category | flops | bytes accessed | tf_op | source)
XLA Modules:
  0.0 343.5 jit_solution(7880529084560656010)
XLA Ops:
  6.5 0.0 copy-start
  6.5 0.0 all-gather.4.cloned.1.call-start
  6.5 6.5 %all-gather = bf16[4,96,512]{2,1,0:T(8,128)(2,1)S(1)} all-gather(bf16[2,96,512]{2,1,0:T(8,128)(2,1)} %param.6), channel_id=2, replica_groups=mesh['band'=64,'ga_0'=2,'ga_1'=2] {'ga_0'}, dimensions={0}, use_global_device_ids=true | all-gather | bytes 589824 | tf_op jit(solution)/shard_map/all_gather | solution.py:19
  13.0 0.0 copy-start.5
  13.0 5.5 %all-gather.1 = bf16[4,2,96,512]{3,2,1,0:T(8,128)(2,1)S(1)} all-gather(bf16[2,2,96,512]{3,2,1,0:T(8,128)(2,1)S(1)} %bitcast.72), channel_id=3, replica_groups=mesh['band'=64,'ga_0'=2,'ga_1'=2] {'ga_1'}, dimensions={0}, use_global_device_ids=true | all-gather | bytes 1179648 | tf_op jit(solution)/shard_map/all_gather | solution.py:19
  18.5 0.1 copy.15
  18.6 0.1 slice_bitcast_fusion
  18.7 0.1 neg.14
  18.8 0.1 maximum_bitcast_fusion.8
  18.9 0.0 copy-done.5
  19.0 0.0 copy-start.2
  19.0 3.7 %fusion.15 = bf16[2,2,96,512]{3,2,1,0:T(8,128)(2,1)} fusion(bf16[2,2,512,2048]{3,2,1,0:T(8,128)(2,1)S(1)} %copy-done.5, bf16[1,2,96,2048]{3,2,1,0:T(8,128)(2,1)S(1)} %get-tuple-element.8, bf16[1,2,96,2048]{3,2,1,0:T(8,128)(2,1)S(1)} %get-tuple-element.7), kind=kOutput, calls=%fused_computation.14 | convolution fusion | flops 1613955072 | bytes 10354688 | tf_op jit(solution)/shard_map/dcmk,wcgk->wdmg/dot_general | solution.py:58
  22.6 0.0 all-gather.4.cloned.1.call-update
  22.7 0.0 copy-done.2
  22.7 0.0 copy-done
  22.7 0.0 copy-start.3
  22.7 0.0 copy-start.4
  22.7 0.0 copy-start.1
  22.7 34.3 %gather_fusion = f32[6144]{0:T(1024)S(1)} fusion(f32[6144]{0:T(1024)S(1)} %copy-done, s32[6144]{0:T(1024)S(1)} %fusion.22), kind=kCustom, calls=%fused_computation | custom fusion | bytes 73728 | tf_op jit(solution)/shard_map/jit(_take)/gather | solution.py:49
  57.0 0.0 copy-done.3
  57.1 0.0 copy-done.4
  57.1 0.1 fusion.21
  57.2 0.1 constant_dynamic-slice_fusion
  57.3 0.0 copy-done.1
  57.3 2.7 add_multiply_fusion
  60.0 223.9 %all-gather.4.cloned.1.call-done = bf16[2,2,6144,512]{3,2,1,0:T(8,128)(2,1)} async-done(((bf16[2,2,96,512]{3,2,1,0:T(8,128)(2,1)}), bf16[2,2,6144,512]{3,2,1,0:T(8,128)(2,1)}) %all-gather.4.cloned.1.call-update) | async-done | bytes 25165840 | tf_op jit(solution)/shard_map/all_gather | solution.py:65
  284.0 16.0 %fusion.2 = bf16[2,96,6144]{2,1,0:T(8,128)(2,1)} fusion(bf16[2,2,6144,512]{3,2,1,0:T(8,128)(2,1)} %all-gather.4.cloned.1.call-done, f32[2,96,6144]{2,1,0:T(8,128)} %add_multiply_fusion, bf16[1,2,96,512]{3,2,1,0:T(8,128)(2,1)S(1)} %maximum_bitcast_fusion.12, bf16[1,2,96,512]{3,2,1,0:T(8,128)(2,1)S(1)} %bitcast.74), kind=kOutput, calls=%fused_computation.4 | convolution fusion | flops 4836163584 | bytes 32636928 | tf_op jit(solution)/shard_map/dcnk,wcmk->wdnm/dot_general | solution.py:62
  300.0 3.5 %convert_element_type.19 = bf16[2,96,4,1536]{3,2,1,0:T(4,128)(2,1)S(1)} reshape(bf16[2,96,6144]{2,1,0:T(8,128)(2,1)} %fusion.2) | data formatting | bytes 4718592 | tf_op jit(solution)/shard_map/convert_element_type | solution.py:70
  303.5 0.4 copy.18
  303.9 31.3 %all_to_all.5 = bf16[4,2,96,1536]{3,2,1,0:T(8,128)(2,1)S(1)} all-to-all(bf16[4,2,96,1536]{3,2,1,0:T(8,128)(2,1)S(1)} %copy.18), channel_id=1, replica_groups=mesh['band'=64,'ga_0'=2,'ga_1'=2] {'ga_0','ga_1'}, dimensions={0} | all-to-all | bytes 4718592 | tf_op jit(solution)/shard_map/all_to_all | solution.py:38
  335.2 1.4 convert_reduce_fusion
  (6 shorter events, 0.1 us)
Async XLA Ops:
  6.5 16.2 %copy-start = (f32[6144]{0:T(1024)S(1)}, f32[6144]{0:T(1024)}, u32[]{:S(2)}) copy-start(f32[6144]{0:T(1024)} %param.8) | copy-start | bytes 73732
  6.5 277.5 %all-gather.4.cloned.1.call-start = ((), (), s32[]{:S(2)}) async-start(), calls=%async_computation.1 | async-start | bytes 25559040 | tf_op jit(solution)/shard_map/all_gather | solution.py:65
  13.0 5.9 %copy-start.5 = (bf16[2,2,512,2048]{3,2,1,0:T(8,128)(2,1)S(1)}, bf16[2,2,512,2048]{3,2,1,0:T(8,128)(2,1)}, u32[]{:S(2)}) copy-start(bf16[2,2,512,2048]{3,2,1,0:T(8,128)(2,1)} %param.7) | copy-start | bytes 25165828
  19.0 3.7 %copy-start.2 = (s32[6144]{0:T(1024)S(1)}, s32[6144]{0:T(1024)}, u32[]{:S(2)}) copy-start(s32[6144]{0:T(1024)} %param.11) | copy-start | bytes 73732
  22.7 34.3 %copy-start.3 = (f32[2]{0:T(128)S(1)}, f32[2]{0:T(128)}, u32[]{:S(2)}) copy-start(f32[2]{0:T(128)} %param.10) | copy-start | bytes 28
  22.7 34.3 %copy-start.4 = (f32[2]{0:T(128)S(1)}, f32[2]{0:T(128)}, u32[]{:S(2)}) copy-start(f32[2]{0:T(128)} %param.9) | copy-start | bytes 28
  22.7 34.5 %copy-start.1 = (bf16[2,96,512]{2,1,0:T(8,128)(2,1)S(1)}, bf16[2,96,512]{2,1,0:T(8,128)(2,1)}, u32[]{:S(2)}) copy-start(bf16[2,96,512]{2,1,0:T(8,128)(2,1)} %param.6) | copy-start | bytes 589828
Sparse Core Ops, SparseCore 0:
  22.8 261.1 all-gather.3
where the time goes:
time: 344 us; the launch traced here: 343 us
  waiting for transfers between devices  224 us (65%)
  blocking collectives  43.3 us (13%)
  local copies, waits for them, and re-layouts  38.5 us (11%)
  matrix products  19.6 us (6%)
  between operations  13.6 us (4%)
  other arithmetic  4.5 us (1%)
    all_gather x1, waiting for transfers between devices, on_device(): lax.all_gather(applied, 'band', axis=2, tiled=True)  224 us
    gather x1, local copies, waits for them, and re-layouts, on_device(): slot_energy = jnp.take(energies, band_of_slot)  34.3 us
    all_to_all x1, blocking collectives, summed_on_arrival(): lax.all_to_all(blocks, axis, split_axis=0, concat_axis=0, tiled=True)  31.3 us
    dot_general x1, matrix products, on_device(): jnp.einsum('dcnk,wcmk->wdnm', left_own, lax.all_gather(applied, 'band', a...  16 us
    all_gather x2, blocking collectives, all_blocks(): blocks = lax.all_gather(blocks, axes[k])  12 us
  transfers between devices with their start and end apart: 1, of which 1 were waited for; matrix products, arithmetic and copies ran while one was open for 11% of the time, Pallas kernels for 0%

commit v1 on v0

--- a/solution.py
+++ b/solution.py
@@ -62,7 +62,9 @@
     pairs = jnp.einsum(
         "dcnk,wcmk->wdnm",
         left_own,
-        lax.all_gather(applied, "band", axis=2, tiled=True),
+        jnp.concatenate(
+            lax.all_to_all(jnp.stack([applied] * lax.axis_size("band")), "band", 0, 0), axis=2
+        ),
         preferred_element_type=jnp.float32,
     )
     factor = 0.5 * (screen_own[:, :, None] + screen[:, None, :])

time: 344 us -> 742 us (2.16)
  the two profiles are of different devices: /device:TPU:1 before, /device:TPU:100 now
where the time goes in v1:
time: 742 us
  waiting for transfers between devices  590 us (80%)
  local copies, waits for them, and re-layouts  70.5 us (10%)
  blocking collectives  41 us (6%)
  matrix products  21.6 us (3%)
  starting transfers between devices  13.6 us (2%)
    all_to_all x1, waiting for transfers between devices, on_device(): lax.all_to_all(jnp.stack([applied] * lax.axis_size('band')), 'band', 0, 0)  590 us
    gather x1, local copies, waits for them, and re-layouts, on_device(): slot_energy = jnp.take(energies, band_of_slot)  34.3 us
    all_to_all x1, blocking collectives, summed_on_arrival(): lax.all_to_all(blocks, axis, split_axis=0, concat_axis=0, tiled=True)  31 us
    reshape x1, local copies, waits for them, and re-layouts, on_device(): jnp.concatenate(lax.all_to_all(jnp.stack([applied] * lax.axis_size('band'...  21.4 us
    dot_general x1, matrix products, on_device(): jnp.einsum('dcnk,wcmk->wdnm', left_own, jnp.concatenate(lax.all_to_all(jn...  15.3 us
  transfers between devices with their start and end apart: 1, of which 1 were waited for; matrix products, arithmetic and copies ran while one was open for 5% of the time, Pallas kernels for 0%

profile of v1, /device:TPU:100, one launch (start us, length us, event | category | flops | bytes accessed | tf_op | source)
XLA Modules:
  0.0 741.6 jit_solution(6393979669843392349)
XLA Ops:
  0.0 0.0 copy-start
  0.0 7.6 %all-gather = bf16[4,96,512]{2,1,0:T(8,128)(2,1)S(1)} all-gather(bf16[2,96,512]{2,1,0:T(8,128)(2,1)} %param.6), channel_id=2, replica_groups=mesh['band'=64,'ga_0'=2,'ga_1'=2] {'ga_0'}, dimensions={0}, use_global_device_ids=true | all-gather | bytes 589824 | tf_op jit(solution)/shard_map/all_gather | solution.py:19
  7.6 2.4 all-gather.1
  10.0 0.8 copy.14
  10.8 0.3 reshape.76
  11.1 0.3 fusion.21
  11.4 0.3 squeeze.4
  11.7 0.1 neg.14
  11.8 0.3 slice.19
  12.0 0.1 maximum_bitcast_fusion.8
  12.2 6.3 fusion.11
  18.5 8.7 %stack.23 = bf16[64,2,2,96,512]{4,3,2,1,0:T(8,128)(2,1)} broadcast(bf16[2,2,96,512]{3,2,1,0:T(8,128)(2,1)S(1)} %copy.15), dimensions={1,2,3,4} | broadcast | bytes 25559040 | tf_op jit(solution)/shard_map/stack | solution.py:66
  27.3 0.0 copy-start.4
  27.3 13.6 %all-to-all-start = ((bf16[64,2,2,96,512]{4,3,2,1,0:T(8,128)(2,1)}), bf16[64,2,2,96,512]{4,3,2,1,0:T(8,128)(2,1)}, u32[]{:S(2)}, u32[]{:S(2)}) async-start(bf16[64,2,2,96,512]{4,3,2,1,0:T(8,128)(2,1)} %stack.23), calls=%async_computation | async-start | bytes 50331648 | tf_op jit(solution)/shard_map/all_to_all | solution.py:66
  40.9 0.0 copy-done.4
  40.9 0.0 copy-done
  40.9 0.0 copy-start.5
  40.9 0.0 copy-start.6
  40.9 0.0 copy-start.3
  41.0 34.3 %gather_fusion = f32[6144]{0:T(1024)S(1)} fusion(f32[6144]{0:T(1024)S(1)} %copy-done, s32[6144]{0:T(1024)S(1)} %fusion.18), kind=kCustom, calls=%fused_computation | custom fusion | bytes 73728 | tf_op jit(solution)/shard_map/jit(_take)/gather | solution.py:49
  75.3 0.0 copy-done.5
  75.3 0.0 copy-done.6
  75.3 0.1 fusion.17
  75.4 0.1 constant_dynamic-slice_fusion
  75.5 0.0 copy-done.3
  75.5 2.8 add_multiply_fusion
  78.3 590.2 %all-to-all-done = bf16[64,2,2,96,512]{4,3,2,1,0:T(8,128)(2,1)} async-done(((bf16[64,2,2,96,512]{4,3,2,1,0:T(8,128)(2,1)}), bf16[64,2,2,96,512]{4,3,2,1,0:T(8,128)(2,1)}, u32[]{:S(2)}, u32[]{:S(2)}) %all-to-all-start) | async-done | bytes 25165856 | tf_op jit(solution)/shard_map/all_to_all | solution.py:66
  668.5 0.0 copy-start.2
  668.5 21.4 %copy.16 = bf16[2,2,64,96,512]{4,3,2,1,0:T(8,128)(2,1)} copy(bf16[2,2,64,96,512]{4,3,1,0,2:T(8,128)(2,1)} %bitcast.12) | data formatting | bytes 50331648 | tf_op jit(solution)/shard_map/reshape | solution.py:65
  689.9 0.0 copy-done.2
  690.0 15.3 %fusion = bf16[2,96,6144]{2,1,0:T(8,128)(2,1)} fusion(bf16[2,2,6144,512,1]{3,2,1,4,0:T(8,128)(2,1)} %bitcast.61, f32[2,96,6144]{2,1,0:T(8,128)S(1)} %copy-done.2, bf16[1,2,96,512]{3,2,1,0:T(8,128)(2,1)S(1)} %maximum_bitcast_fusion.12, bf16[1,2,96,512]{3,2,1,0:T(8,128)(2,1)S(1)} %bitcast.66), kind=kOutput, calls=%fused_computation.2 | convolution fusion | flops 4836163584 | bytes 32636928 | tf_op jit(solution)/shard_map/dcnk,wcmk->wdnm/dot_general | solution.py:62
  705.3 3.5 convert_element_type.19
  708.8 0.0 copy-start.1
  708.8 0.4 copy.17
  709.3 31.0 %all_to_all.10 = bf16[4,2,96,1536]{3,2,1,0:T(8,128)(2,1)S(1)} all-to-all(bf16[4,2,96,1536]{3,2,1,0:T(8,128)(2,1)S(1)} %copy.17), channel_id=1, replica_groups=mesh['band'=64,'ga_0'=2,'ga_1'=2] {'ga_0','ga_1'}, dimensions={0} | all-to-all | bytes 4718592 | tf_op jit(solution)/shard_map/all_to_all | solution.py:38
  740.2 1.4 convert_reduce_fusion
  741.6 0.0 copy-done.1
  (5 shorter events, 0.1 us)
Async XLA Ops:
  0.0 40.9 %copy-start = (f32[6144]{0:T(1024)S(1)}, f32[6144]{0:T(1024)}, u32[]{:S(2)}) copy-start(f32[6144]{0:T(1024)} %param.8) | copy-start | bytes 73732
  27.3 13.6 %copy-start.4 = (s32[6144]{0:T(1024)S(1)}, s32[6144]{0:T(1024)}, u32[]{:S(2)}) copy-start(s32[6144]{0:T(1024)} %param.11) | copy-start | bytes 73732
  27.3 641.2 %all-to-all-start = ((bf16[64,2,2,96,512]{4,3,2,1,0:T(8,128)(2,1)}), bf16[64,2,2,96,512]{4,3,2,1,0:T(8,128)(2,1)}, u32[]{:S(2)}, u32[]{:S(2)}) async-start(bf16[64,2,2,96,512]{4,3,2,1,0:T(8,128)(2,1)} %stack.23), calls=%async_computation | async-start | bytes 50331648 | tf_op jit(solution)/shard_map/all_to_all | solution.py:66
  40.9 34.3 %copy-start.5 = (f32[2]{0:T(128)S(1)}, f32[2]{0:T(128)}, u32[]{:S(2)}) copy-start(f32[2]{0:T(128)} %param.10) | copy-start | bytes 28
  40.9 34.3 %copy-start.6 = (f32[2]{0:T(128)S(1)}, f32[2]{0:T(128)}, u32[]{:S(2)}) copy-start(f32[2]{0:T(128)} %param.9) | copy-start | bytes 28
  40.9 34.5 %copy-start.3 = (bf16[2,96,512]{2,1,0:T(8,128)(2,1)S(1)}, bf16[2,96,512]{2,1,0:T(8,128)(2,1)}, u32[]{:S(2)}) copy-start(bf16[2,96,512]{2,1,0:T(8,128)(2,1)} %param.6) | copy-start | bytes 589828
  668.5 21.4 %copy-start.2 = (f32[2,96,6144]{2,1,0:T(8,128)S(1)}, f32[2,96,6144]{2,1,0:T(8,128)}, u32[]{:S(2)}) copy-start(f32[2,96,6144]{2,1,0:T(8,128)} %add_multiply_fusion) | copy-start | bytes 14155780
  708.8 32.8 %copy-start.1 = (f32[6144]{0:T(1024)S(1)}, f32[6144]{0:T(1024)}, u32[]{:S(2)}) copy-start(f32[6144]{0:T(1024)} %param.8) | copy-start | bytes 73732
